TPU v7x, 32 devices: a whole 2x2x4 slice. The times are simulated.
32 devices in a mesh: row: 8 (over z, core), col: 4 (over y, x).
Axes of the slice: x: 2, y: 2, z: 4, core: 2. Of those that a mesh axis runs over, the one named last changes fastest.
Arguments:
- matrix: float32 [1728, 65536], P('row', 'col'), may hold values from -6 to 6
- range_basis: float32 [1728, 384], P('col', 'row'), may hold values from -0.21875 to 0.21875
Outputs:
- projected: float32 [384, 65536], P('row')
All inputs are finite; a program needn't handle non-finite values.
Results may differ from a plain program's by a relative error of at most 0.000071.
Values sent between devices are 32-bit elements; how exact they have to be, the bound alone decides.
A program may use at most 128 MiB of HBM per device.

v0:
```python
import jax
import jax.numpy as jnp
from jax import lax
from jax.experimental import pallas as pl
from jax.experimental.pallas import tpu as pltpu
from jax.sharding import PartitionSpec as P

MESH = pl.DeviceIdType.MESH
CHUNKS = 8
CORES = 2


def split_parts(value):
    high = value.astype(jnp.bfloat16)
    return high, (value - high.astype(jnp.float32)).astype(jnp.bfloat16)


def kernel(
    chips, cols, basis_ref, matrix_ref, out_ref, basis, halves, rows, part, sums,
    basis_send, basis_recv, rows_local, rows_send, rows_recv, sum_send, sum_recv, out_send, out_recv,
):
    row, col = lax.axis_index("row"), lax.axis_index("col")
    chip, core = row // CORES, row % CORES
    vectors = basis_ref.shape[0]
    depth = matrix_ref.shape[0]
    chunks, _, width = rows.shape
    block = matrix_ref.shape[1]

    def basis_copy(target):
        return pltpu.make_async_remote_copy(
            src_ref=basis_ref,
            dst_ref=basis.at[pl.ds(chip * vectors, vectors)],
            send_sem=basis_send.at[target],
            recv_sem=basis_recv.at[chip],
            device_id={"row": CORES * col + core, "col": target},
            device_id_type=MESH,
        )

    def basis_own():
        return pltpu.make_async_copy(
            basis_ref, basis.at[pl.ds(chip * vectors, vectors)], basis_recv.at[chip]
        )

    def rows_own(step):
        return pltpu.make_async_copy(
            matrix_ref.at[:, pl.ds(step * width, width)],
            rows.at[step, pl.ds(core * depth, depth)],
            rows_local.at[step],
        )

    def rows_peer(step, owner):
        return pltpu.make_async_remote_copy(
            src_ref=matrix_ref.at[:, pl.ds(step * width, width)],
            dst_ref=rows.at[step, pl.ds(owner * depth, depth)],
            send_sem=rows_send.at[step],
            recv_sem=rows_recv.at[step],
            device_id={"row": CORES * chip + 1 - core, "col": col},
            device_id_type=MESH,
        )

    def sum_copy(source, owner, slot, step, towards):
        return pltpu.make_async_remote_copy(
            src_ref=source,
            dst_ref=sums.at[slot, step],
            send_sem=sum_send.at[owner, step],
            recv_sem=sum_recv.at[slot, step],
            device_id={"row": CORES * towards + core, "col": col},
            device_id_type=MESH,
        )

    def part_of(step, owner):
        return part.at[step, pl.ds(owner * vectors, vectors)]

    def send_up(source, owner, step):
        sum_copy(source, owner, owner, step, chip + 1).start()

    def send_down(source, owner, step):
        slot = jnp.where(owner == chip - 1, chips, owner)
        sum_copy(source, owner, slot, step, chip - 1).start()

    def sum_wait(slot, step):
        neighbour = jnp.where(chip == 0, 1, chip - 1)
        sum_copy(sums.at[slot, step], 0, slot, step, neighbour).wait_recv()

    def out_at(step, owner):
        return out_ref.at[:, pl.ds(owner * block + step * width, width)]

    def out_copy(step, target):
        return pltpu.make_async_remote_copy(
            src_ref=part_of(step, chip),
            dst_ref=out_at(step, col),
            send_sem=out_send.at[target, step],
            recv_sem=out_recv.at[col, step],
            device_id={"row": row, "col": target},
            device_id_type=MESH,
        )

    def out_wait(step, source):
        pltpu.make_async_remote_copy(
            src_ref=part_of(step, chip),
            dst_ref=out_at(step, source),
            send_sem=out_send.at[source, step],
            recv_sem=out_recv.at[source, step],
            device_id={"row": row, "col": source},
            device_id_type=MESH,
        ).wait_recv()

    def out_own(step):
        return pltpu.make_async_copy(part_of(step, chip), out_at(step, col), out_recv.at[col, step])

    for shift in range(cols):
        target = lax.rem(col + shift, cols)
        if shift:
            basis_copy(target).start()
        else:
            pl.when(chip == col)(lambda: basis_own().start())
            pl.when(chip != col)(lambda: basis_copy(col).start())

    @pl.loop(0, chunks)
    def _(step):
        rows_peer(step, core).start()
        rows_own(step).start()

    for source in range(chips):
        pltpu.make_async_copy(
            basis_ref, basis.at[pl.ds(source * vectors, vectors)], basis_recv.at[source]
        ).wait()
    high, low = split_parts(basis[...])
    count = chips * vectors
    halves[:count] = high
    halves[count:] = low

    tile = min(256, width)

    @pl.loop(0, chunks)
    def _(step):
        rows_own(step).wait()
        rows_peer(step, 1 - core).wait_recv()

        @pl.loop(0, width // tile)
        def _(at):
            lanes = pl.ds(pl.multiple_of(at * tile, tile), tile)
            right, rest = split_parts(rows[step, :, lanes])
            inner = CORES * depth
            both = jnp.dot(halves[:, :inner], right, preferred_element_type=jnp.float32)
            third = jnp.dot(halves[:count, :inner], rest, preferred_element_type=jnp.float32)
            part[step, :, lanes] = both[:count] + (both[count:] + third)

        @pl.when(chip == 0)
        def _():
            for owner in range(chips - 1, 0, -1):
                send_up(part_of(step, owner), owner, step)

        @pl.when(chip == chips - 1)
        def _():
            for owner in range(chips - 1):
                send_down(part_of(step, owner), owner, step)

    def add(step, slot, owner):
        at = pl.ds(pl.multiple_of(owner * vectors, vectors), vectors)
        return sums[slot, step] + part[step, at]

    @pl.loop(0, chunks)
    def _(step):
        for owner in range(chips - 1, 0, -1):

            @pl.when((chip > 0) & (chip < owner))
            def _():
                sum_wait(owner, step)
                sums[owner, step] = add(step, owner, owner)
                send_up(sums.at[owner, step], owner, step)

            down = chips - 1 - owner

            @pl.when((chip < chips - 1) & (chip > down))
            def _():
                sum_wait(down, step)
                sums[down, step] = add(step, down, down)
                send_down(sums.at[down, step], down, step)

        mine = pl.ds(pl.multiple_of(chip * vectors, vectors), vectors)

        @pl.when(chip > 0)
        def _():
            sum_wait(chip, step)
            part[step, mine] = sums[chip, step] + part[step, mine]

        @pl.when(chip < chips - 1)
        def _():
            sum_wait(chips, step)
            part[step, mine] = sums[chips, step] + part[step, mine]

        for shift in range(1, cols):
            out_copy(step, lax.rem(col + shift, cols)).start()
        out_own(step).start()

    for shift in range(cols):
        target = lax.rem(col + shift, cols)
        if shift:
            basis_copy(target).wait_send()
        else:
            pl.when(chip != col)(lambda: basis_copy(col).wait_send())

    @pl.loop(0, chunks)
    def _(step):
        rows_peer(step, core).wait_send()
        for owner in range(chips):
            neighbour = jnp.where(chip == 0, 1, chip - 1)

            @pl.when(owner != chip)
            def _():
                sum_copy(part_of(step, owner), owner, owner, step, neighbour).wait_send()

        for shift in range(1, cols):
            other = lax.rem(col + shift, cols)
            out_copy(step, other).wait_send()
            out_wait(step, other)
        out_own(step).wait()


def solution(mesh):
    chips, cols = mesh.shape["row"] // CORES, mesh.shape["col"]

    def per_device(matrix, range_basis):
        depth, block = matrix.shape
        inner, vectors = range_basis.shape
        assert chips == cols and inner == CORES * depth
        padded = -(-inner // 128) * 128
        width = block // CHUNKS
        mine = jnp.pad(range_basis.T, ((0, 0), (0, padded - inner)))
        count = chips * vectors
        dma = pltpu.SemaphoreType.DMA
        return pl.pallas_call(
            lambda *refs: kernel(chips, cols, *refs),
            out_shape=jax.ShapeDtypeStruct((vectors, cols * block), jnp.float32),
            in_specs=[
                pl.BlockSpec(memory_space=pltpu.VMEM),
                pl.BlockSpec(memory_space=pl.ANY),
            ],
            out_specs=pl.BlockSpec(memory_space=pl.ANY),
            scratch_shapes=[
                pltpu.VMEM((count, padded), jnp.float32),
                pltpu.VMEM((2 * count, padded), jnp.bfloat16),
                pltpu.VMEM((CHUNKS, inner, width), jnp.float32),
                pltpu.VMEM((CHUNKS, count, width), jnp.float32),
                pltpu.VMEM((chips + 1, CHUNKS, vectors, width), jnp.float32),
                dma((cols,)),
                dma((chips,)),
                dma((CHUNKS,)),
                dma((CHUNKS,)),
                dma((CHUNKS,)),
                dma((chips, CHUNKS)),
                dma((chips + 1, CHUNKS)),
                dma((cols, CHUNKS)),
                dma((cols, CHUNKS)),
            ],
            compiler_params=pltpu.CompilerParams(
                has_side_effects=True, vmem_limit_bytes=66_000_000
            ),
        )(mine, matrix)

    return jax.shard_map(
        per_device,
        mesh=mesh,
        in_specs=(P("row", "col"), P("col", "row")),
        out_specs=P("row", None),
        check_vma=False,
    )
```

profile of v0, /device:TPU:0, one launch (start us, length us, event | category | flops | bytes accessed | tf_op | source)
XLA Modules:
  0.0 286.8 jit_solution(9943430525350339653)
XLA Ops:
  0.0 1.5 pad.4.refs_0_
  1.5 275.0 %shard_map.28 = f32[48,65536]{1,0:T(8,128)} custom-call(f32[48,512]{1,0:T(8,128)} %pad.4.refs_0_, f32[216,16384]{1,0:T(8,128)} %refs_1_.1), custom_call_target="tpu_custom_call" | custom-call | tf_op jit(solution)/shard_map/pallas_call | solution.py:233
  276.6 10.2 %copy.4 = f32[48,65536]{1,0:T(8,128)} copy(f32[48,65536]{1,0:T(8,128)} %shard_map.28) | data formatting | bytes 25165824
where the time goes:
time: 288 us; the launch traced here: 287 us
  Pallas kernels  275 us (95%)
  local copies, waits for them, and re-layouts  11.7 us (4%)
    pallas_call x1, Pallas kernels, per_device(): pl.pallas_call(lambda *refs: kernel(chips, cols, *refs), out_shape=jax.Sh...  275 us
    unnamed x1, local copies, waits for them, and re-layouts  10.2 us

commit v1 on v0

v1 whole, which is shorter than its diff:
```python
import functools

import jax
import jax.numpy as jnp
from jax import lax
from jax.experimental import pallas as pl
from jax.experimental.pallas import tpu as pltpu
from jax.sharding import PartitionSpec as P

MESH = pl.DeviceIdType.MESH
CORES = 2
WIDTH = 512
LEAD = 4
SKEW = 1
SPARE = 3
AHEAD = 3


def split_parts(value):
    high = value.astype(jnp.bfloat16)
    return high, (value - high.astype(jnp.float32)).astype(jnp.bfloat16)


def dot(left, right):
    return jnp.dot(left, right, preferred_element_type=jnp.float32)


def kernel(
    chips, cols, basis_ref, matrix_ref, out_ref, mine_basis, basis, halves, rows, part, sums,
    basis_load, basis_send, basis_recv, rows_local, rows_send, rows_recv,
    sum_send, sum_recv, out_send, out_recv,
):
    row, col = lax.axis_index("row"), lax.axis_index("col")
    chip, core = row // CORES, row % CORES
    vectors, inner = basis_ref.shape
    depth, block = matrix_ref.shape
    steps, _, width = rows.shape
    count = chips * vectors
    tile = min(256, width)
    first, last = chip == 0, chip == chips - 1
    ends = first | last
    ring = part.shape[0]

    def device(at_chip, at_col, at_core=core):
        return {"row": CORES * at_chip + at_core, "col": at_col}

    def basis_copy(target):
        return pltpu.make_async_remote_copy(
            src_ref=mine_basis,
            dst_ref=basis.at[chip],
            send_sem=basis_send.at[target],
            recv_sem=basis_recv.at[chip],
            device_id=device(col, target),
            device_id_type=MESH,
        )

    def basis_own():
        return pltpu.make_async_copy(basis_ref, basis.at[chip], basis_recv.at[chip])

    def basis_wait(source):
        pltpu.make_async_copy(basis_ref, basis.at[source], basis_recv.at[source]).wait()

    def rows_own(step):
        return pltpu.make_async_copy(
            matrix_ref.at[:, pl.ds(step * width, width)],
            rows.at[step, pl.ds(core * depth, depth)],
            rows_local.at[step],
        )

    def rows_peer(step, owner):
        return pltpu.make_async_remote_copy(
            src_ref=matrix_ref.at[:, pl.ds(step * width, width)],
            dst_ref=rows.at[step, pl.ds(owner * depth, depth)],
            send_sem=rows_send.at[step],
            recv_sem=rows_recv.at[step],
            device_id=device(chip, col, 1 - core),
            device_id_type=MESH,
        )

    def sum_copy(source, owner, slot, step, towards):
        return pltpu.make_async_remote_copy(
            src_ref=source,
            dst_ref=sums.at[slot, step],
            send_sem=sum_send.at[owner, step],
            recv_sem=sum_recv.at[slot, step],
            device_id=device(towards, col),
            device_id_type=MESH,
        )

    def owned(owner):
        return pl.ds(pl.multiple_of(owner * vectors, vectors), vectors)

    def part_of(step, owner):
        return part.at[lax.rem(step, ring), owned(owner)]

    def send_up(source, owner, step):
        sum_copy(source, owner, owner, step, chip + 1).start()

    def send_down(source, owner, step):
        slot = jnp.where(owner == chip - 1, chips, owner)
        sum_copy(source, owner, slot, step, chip - 1).start()

    neighbour = jnp.where(first, 1, chip - 1)

    def sum_wait(slot, step):
        sum_copy(sums.at[slot, step], 0, slot, step, neighbour).wait_recv()

    def sums_sent(step):
        for owner in range(chips):

            @pl.when(owner != chip)
            def _():
                sum_copy(sums.at[owner, step], owner, owner, step, neighbour).wait_send()

    def out_at(step, owner):
        return out_ref.at[:, pl.ds(pl.multiple_of(owner * block + step * width, width), width)]

    def out_copy(step, target, owner):
        return pltpu.make_async_remote_copy(
            src_ref=out_at(step, col),
            dst_ref=out_at(step, owner),
            send_sem=out_send.at[target, step],
            recv_sem=out_recv.at[owner, step],
            device_id=device(chip, target),
            device_id_type=MESH,
        )

    load = pltpu.make_async_copy(basis_ref, mine_basis, basis_load)
    load.start()
    for step in range(AHEAD):
        rows_own(step).start()

    barrier = pltpu.get_barrier_semaphore()

    def greet(where):
        pl.semaphore_signal(barrier, inc=1, device_id=where, device_id_type=MESH)

    greet(device(chip, col, 1 - core))
    for source in range(chips):
        pl.when((source != chip) | (col != chip))(lambda: greet(device(source, chip)))
    pl.when(chip > 0)(lambda: greet(device(chip - 1, col)))
    pl.when(chip < chips - 1)(lambda: greet(device(chip + 1, col)))
    for shift in range(1, cols):
        greet(device(chip, lax.rem(col + shift, cols)))
    greeted = 1 + chips - jnp.where(col == chip, 1, 0) + 2 - jnp.where(ends, 1, 0) + cols - 1
    load.wait()
    pl.when(chip == col)(lambda: basis_own().start())
    pl.semaphore_wait(barrier, greeted)

    for shift in range(cols):
        target = lax.rem(col + shift, cols)
        if shift:
            basis_copy(target).start()
        else:
            pl.when(chip != col)(lambda: basis_copy(col).start())
    for step in range(AHEAD):
        rows_peer(step, core).start()

    def fetch(step):
        @pl.when(step < steps)
        def _():
            rows_own(step).start()
            rows_peer(step, core).start()

    def rows_ready(step):
        rows_own(step).wait()
        rows_peer(step, 1 - core).wait_recv()

    def tiles(body):
        @pl.loop(0, width // tile)
        def _(at):
            body(pl.ds(pl.multiple_of(at * tile, tile), tile))

    rows_ready(0)
    way = jnp.where(chip < chips // 2, 1, chips - 1)
    for hop in range(1, chips + 1):
        owner = lax.rem(chip + hop * way, chips)
        basis_wait(owner)

        @functools.partial(tiles)
        def _(lanes):
            right, rest = split_parts(rows[0, :, lanes])
            high, low = split_parts(basis[owner])
            part[0, owned(owner), lanes] = dot(high, right) + (dot(low, right) + dot(high, rest))

        if hop < chips:
            pl.when(first)(lambda: send_up(part_of(0, owner), owner, 0))
            pl.when(last)(lambda: send_down(part_of(0, owner), owner, 0))

    high, low = split_parts(basis[...].reshape(count, inner))
    halves[:count, :inner] = high
    halves[count:, :inner] = low

    def compute(step):
        fetch(step + AHEAD - 1)
        rows_ready(step)
        slot = lax.rem(step, ring)

        @pl.when(ends & (step >= ring))
        def _():
            sums_sent(step - ring)

        @functools.partial(tiles)
        def _(lanes):
            right, rest = split_parts(rows[step, :, lanes])
            both = dot(halves[:, :inner], right)
            third = dot(halves[:count, :inner], rest)
            part[slot, :, lanes] = both[:count] + (both[count:] + third)

    def launch(tick):
        for far in range(chips - 1):
            step = tick - SKEW * far

            @pl.when((step > 0) & (step < steps))
            def _():
                up, down = chips - 1 - far, far
                pl.when(first)(lambda: send_up(part_of(step, up), up, step))
                pl.when(last)(lambda: send_down(part_of(step, down), down, step))

    @pl.loop(1, LEAD)
    def _(step):
        compute(step)
        launch(step)

    def forward(owner, step, send):
        @pl.when((step >= 0) & (step < steps))
        def _():
            sum_wait(owner, step)
            sums[owner, step] = sums[owner, step] + part[lax.rem(step, ring), owned(owner)]
            send(sums.at[owner, step], owner, step)

    @pl.loop(0, steps + SKEW * (chips - 1))
    def _(turn):
        pl.when(turn + LEAD < steps)(lambda: compute(turn + LEAD))
        launch(turn + LEAD)

        for owner in range(chips - 1, 0, -1):
            step = turn - SKEW * (chip + chips - 1 - owner)
            pl.when((chip > 0) & (chip < owner))(lambda: forward(owner, step, send_up))
            down = chips - 1 - owner
            back = turn - SKEW * (chips - 1 - chip + down)
            pl.when((chip < chips - 1) & (chip > down))(lambda: forward(down, back, send_down))

        @pl.when(turn >= SKEW * (chips - 1))
        def _():
            step = turn - SKEW * (chips - 1)
            slot = lax.rem(step, ring)
            here = pl.ds(pl.multiple_of(col * block + step * width, width), width)

            @pl.when(first)
            def _():
                sum_wait(chips, step)
                out_ref[:, here] = sums[chips, step] + part[slot, owned(chip)]

            @pl.when(last)
            def _():
                sum_wait(chip, step)
                out_ref[:, here] = sums[chip, step] + part[slot, owned(chip)]

            @pl.when(jnp.logical_not(ends))
            def _():
                sum_wait(chip, step)
                sum_wait(chips, step)
                out_ref[:, here] = sums[chip, step] + (sums[chips, step] + part[slot, owned(chip)])

            for shift in range(1, cols):
                out_copy(step, lax.rem(col + shift, cols), col).start()

    for shift in range(cols):
        target = lax.rem(col + shift, cols)
        if shift:
            basis_copy(target).wait_send()
        else:
            pl.when(chip != col)(lambda: basis_copy(col).wait_send())

    @pl.loop(0, steps)
    def _(step):
        rows_peer(step, core).wait_send()
        pl.when(jnp.logical_not(ends) | (step >= steps - ring))(lambda: sums_sent(step))
        for shift in range(1, cols):
            other = lax.rem(col + shift, cols)
            out_copy(step, other, col).wait_send()
            out_copy(step, other, other).wait_recv()


def solution(mesh):
    chips, cols = mesh.shape["row"] // CORES, mesh.shape["col"]

    def per_device(matrix, range_basis):
        depth, block = matrix.shape
        inner, vectors = range_basis.shape
        assert chips == cols and inner == CORES * depth and block % WIDTH == 0
        steps = block // WIDTH
        ring = LEAD + SKEW * (chips - 1) + SPARE
        padded = -(-inner // 128) * 128
        count = chips * vectors
        dma = pltpu.SemaphoreType.DMA
        return pl.pallas_call(
            functools.partial(kernel, chips, cols),
            out_shape=pltpu.VMEM((vectors, cols * block), jnp.float32),
            in_specs=[pl.BlockSpec(memory_space=pl.ANY)] * 2,
            out_specs=pl.BlockSpec(memory_space=pltpu.VMEM),
            scratch_shapes=[
                pltpu.VMEM((vectors, inner), jnp.float32),
                pltpu.VMEM((chips, vectors, inner), jnp.float32),
                pltpu.VMEM((2 * count, padded), jnp.bfloat16),
                pltpu.VMEM((steps, inner, WIDTH), jnp.float32),
                pltpu.VMEM((ring, count, WIDTH), jnp.float32),
                pltpu.VMEM((chips + 1, steps, vectors, WIDTH), jnp.float32),
                dma,
                dma((cols,)),
                dma((chips,)),
                dma((steps,)),
                dma((steps,)),
                dma((steps,)),
                dma((chips, steps)),
                dma((chips + 1, steps)),
                dma((cols, steps)),
                dma((cols, steps)),
            ],
            compiler_params=pltpu.CompilerParams(
                has_side_effects=True, collective_id=0, vmem_limit_bytes=52_000_000
            ),
        )(range_basis.T, matrix)

    return jax.shard_map(
        per_device,
        mesh=mesh,
        in_specs=(P("row", "col"), P("col", "row")),
        out_specs=P("row", None),
        check_vma=False,
    )
```

time: 288 us -> 253 us (0.88)
  Pallas kernels: 275 us -> 245 us
  local copies, waits for them, and re-layouts: 11.7 us -> 4.78 us
    pallas_call x1, Pallas kernels: 275 us -> 245 us  [per_device(): pl.pallas_call(functools.partial(kernel, chips, cols), out_shape=pltpu.VM...]
    unnamed x1, local copies, waits for them, and re-layouts: 10.2 us -> 4.78 us
where the time goes in v1:
time: 253 us; the launch traced here: 250 us
  Pallas kernels  245 us (97%)
  local copies, waits for them, and re-layouts  4.78 us (2%)
    pallas_call x1, Pallas kernels, per_device(): pl.pallas_call(functools.partial(kernel, chips, cols), out_shape=pltpu.VM...  245 us

profile of v1, /device:TPU:0, one launch (start us, length us, event | category | flops | bytes accessed | tf_op | source)
XLA Modules:
  0.0 249.6 jit_solution(14650549237290299020)
XLA Ops:
  0.0 244.8 %shard_map.28 = f32[48,65536]{1,0:T(8,128)S(1)} custom-call(f32[48,432]{1,0:T(8,128)} %bitcast.1, f32[216,16384]{1,0:T(8,128)} %matrix_ref.1), custom_call_target="tpu_custom_call" | custom-call | tf_op jit(solution)/shard_map/pallas_call | solution.py:298
  244.8 4.8 %copy.4 = f32[48,65536]{1,0:T(8,128)} copy(f32[48,65536]{1,0:T(8,128)S(1)} %shard_map.28) | data formatting | bytes 25165824

commit v2 on v1

--- a/solution.py
+++ b/solution.py
@@ -13,7 +13,7 @@
 LEAD = 4
 SKEW = 1
 SPARE = 3
-AHEAD = 3
+AHEAD = 6
 
 
 def split_parts(value):
@@ -26,8 +26,8 @@
 
 
 def kernel(
-    chips, cols, basis_ref, matrix_ref, out_ref, mine_basis, basis, halves, rows, part, sums,
-    basis_load, basis_send, basis_recv, rows_local, rows_send, rows_recv,
+    chips, cols, basis_ref, matrix_ref, out_ref, loaded, cut, relay, basis, halves, rows, part, sums,
+    basis_load, cut_send, cut_recv, line_send, spread_send, basis_recv, rows_local, rows_send, rows_recv,
     sum_send, sum_recv, out_send, out_recv,
 ):
     row, col = lax.axis_index("row"), lax.axis_index("col")
@@ -44,21 +44,43 @@
     def device(at_chip, at_col, at_core=core):
         return {"row": CORES * at_chip + at_core, "col": at_col}
 
-    def basis_copy(target):
-        return pltpu.make_async_remote_copy(
-            src_ref=mine_basis,
-            dst_ref=basis.at[chip],
-            send_sem=basis_send.at[target],
-            recv_sem=basis_recv.at[chip],
-            device_id=device(col, target),
-            device_id_type=MESH,
-        )
-
-    def basis_own():
-        return pltpu.make_async_copy(basis_ref, basis.at[chip], basis_recv.at[chip])
-
-    def basis_wait(source):
-        pltpu.make_async_copy(basis_ref, basis.at[source], basis_recv.at[source]).wait()
+    cuts = cut.shape[0]
+
+    def cut_copy(target):
+        return pltpu.make_async_remote_copy(
+            src_ref=cut.at[target],
+            dst_ref=relay.at[col],
+            send_sem=cut_send.at[target],
+            recv_sem=cut_recv.at[col],
+            device_id=device(chip, target),
+            device_id_type=MESH,
+        )
+
+    def cut_wait(source):
+        pltpu.make_async_copy(cut.at[0], relay.at[source], cut_recv.at[source]).wait()
+
+    def line_copy(plane):
+        return pltpu.make_async_remote_copy(
+            src_ref=relay.at[plane],
+            dst_ref=basis.at[chip, col],
+            send_sem=line_send.at[plane],
+            recv_sem=basis_recv.at[chip, col],
+            device_id=device(plane, col),
+            device_id_type=MESH,
+        )
+
+    def spread_copy(source, owner, target):
+        return pltpu.make_async_remote_copy(
+            src_ref=source,
+            dst_ref=basis.at[owner, col],
+            send_sem=spread_send.at[owner, target],
+            recv_sem=basis_recv.at[owner, col],
+            device_id=device(chip, target),
+            device_id_type=MESH,
+        )
+
+    def basis_wait(owner, at):
+        pltpu.make_async_copy(cut.at[0], basis.at[owner, at], basis_recv.at[owner, at]).wait()
 
     def rows_own(step):
         return pltpu.make_async_copy(
@@ -125,7 +147,7 @@
             device_id_type=MESH,
         )
 
-    load = pltpu.make_async_copy(basis_ref, mine_basis, basis_load)
+    load = pltpu.make_async_copy(basis_ref, loaded, basis_load)
     load.start()
     for step in range(AHEAD):
         rows_own(step).start()
@@ -135,25 +157,56 @@
     def greet(where):
         pl.semaphore_signal(barrier, inc=1, device_id=where, device_id_type=MESH)
 
-    greet(device(chip, col, 1 - core))
-    for source in range(chips):
-        pl.when((source != chip) | (col != chip))(lambda: greet(device(source, chip)))
-    pl.when(chip > 0)(lambda: greet(device(chip - 1, col)))
-    pl.when(chip < chips - 1)(lambda: greet(device(chip + 1, col)))
+    for plane in range(chips):
+        pl.when(plane != chip)(lambda: greet(device(plane, col)))
     for shift in range(1, cols):
         greet(device(chip, lax.rem(col + shift, cols)))
-    greeted = 1 + chips - jnp.where(col == chip, 1, 0) + 2 - jnp.where(ends, 1, 0) + cols - 1
+    greet(device(chip, col, 1 - core))
     load.wait()
-    pl.when(chip == col)(lambda: basis_own().start())
-    pl.semaphore_wait(barrier, greeted)
-
-    for shift in range(cols):
+    for at in range(cuts):
+        size = min(128, inner - at * 128)
+        cut[at, :, :size] = loaded[:, at * 128 : at * 128 + size]
+        if size < 128:
+            cut[at, :, size:] = jnp.zeros((vectors, 128 - size), jnp.float32)
+
+    relays = col < cuts
+
+    @pl.when(relays)
+    def _():
+        relay[col] = cut[lax.rem(col, cuts)]
+
+    pl.semaphore_wait(barrier, chips + cols - 1)
+
+    for shift in range(1, cols):
         target = lax.rem(col + shift, cols)
-        if shift:
-            basis_copy(target).start()
-        else:
-            pl.when(chip != col)(lambda: basis_copy(col).start())
-    for step in range(AHEAD):
+        pl.when(target < cuts)(lambda: cut_copy(target).start())
+    rows_peer(0, core).start()
+
+    low_half = chip < chips // 2
+    way = jnp.where(low_half, 1, chips - 1)
+
+    @pl.when(relays)
+    def _():
+        for hop in range(chips):
+            plane = jnp.where(low_half, hop, chips - 1 - hop)
+            pl.when(plane != col)(lambda: cut_wait(plane))
+            pl.when(plane != chip)(lambda: line_copy(plane).start())
+
+    rows_peer(1, core).start()
+
+    @pl.when(relays)
+    def _():
+        for hop in range(1, chips + 1):
+            owner = lax.rem(chip + hop * way, chips)
+            if hop < chips:
+                basis_wait(owner, col)
+            else:
+                basis[owner, col] = relay[owner]
+            source = basis.at[owner, col] if hop < chips else relay.at[owner]
+            for shift in range(1, cols):
+                spread_copy(source, owner, lax.rem(col + shift, cols)).start()
+
+    for step in range(2, AHEAD):
         rows_peer(step, core).start()
 
     def fetch(step):
@@ -171,28 +224,34 @@
         def _(at):
             body(pl.ds(pl.multiple_of(at * tile, tile), tile))
 
-    rows_ready(0)
-    way = jnp.where(chip < chips // 2, 1, chips - 1)
     for hop in range(1, chips + 1):
         owner = lax.rem(chip + hop * way, chips)
-        basis_wait(owner)
-
-        @functools.partial(tiles)
-        def _(lanes):
-            right, rest = split_parts(rows[0, :, lanes])
-            high, low = split_parts(basis[owner])
-            part[0, owned(owner), lanes] = dot(high, right) + (dot(low, right) + dot(high, rest))
-
-        if hop < chips:
-            pl.when(first)(lambda: send_up(part_of(0, owner), owner, 0))
-            pl.when(last)(lambda: send_down(part_of(0, owner), owner, 0))
-
-    high, low = split_parts(basis[...].reshape(count, inner))
-    halves[:count, :inner] = high
-    halves[count:, :inner] = low
+        for at in range(cuts):
+            pl.when(col != at)(lambda: basis_wait(owner, at))
+
+        @pl.loop(0, LEAD)
+        def _(step):
+            if hop == 1:
+                rows_ready(step)
+
+            @functools.partial(tiles)
+            def _(lanes):
+                right, rest = split_parts(rows[step, :, lanes])
+                mine = jnp.concatenate([basis[owner, at] for at in range(cuts)], axis=1)
+                high, low = split_parts(mine[:, :inner])
+                part[step, owned(owner), lanes] = dot(high, right) + (dot(low, right) + dot(high, rest))
+
+            if hop < chips:
+                pl.when(first)(lambda: send_up(part_of(step, owner), owner, step))
+                pl.when(last)(lambda: send_down(part_of(step, owner), owner, step))
+
+    whole = [basis[:, at].reshape(count, 128) for at in range(cuts)]
+    high, low = split_parts(jnp.concatenate(whole, axis=1))
+    halves[:count] = high
+    halves[count:] = low
 
     def compute(step):
-        fetch(step + AHEAD - 1)
+        fetch(step + AHEAD - LEAD)
         rows_ready(step)
         slot = lax.rem(step, ring)
 
@@ -211,16 +270,11 @@
         for far in range(chips - 1):
             step = tick - SKEW * far
 
-            @pl.when((step > 0) & (step < steps))
+            @pl.when((step >= LEAD) & (step < steps))
             def _():
                 up, down = chips - 1 - far, far
                 pl.when(first)(lambda: send_up(part_of(step, up), up, step))
                 pl.when(last)(lambda: send_down(part_of(step, down), down, step))
-
-    @pl.loop(1, LEAD)
-    def _(step):
-        compute(step)
-        launch(step)
 
     def forward(owner, step, send):
         @pl.when((step >= 0) & (step < steps))
@@ -266,12 +320,16 @@
             for shift in range(1, cols):
                 out_copy(step, lax.rem(col + shift, cols), col).start()
 
-    for shift in range(cols):
+    for shift in range(1, cols):
         target = lax.rem(col + shift, cols)
-        if shift:
-            basis_copy(target).wait_send()
-        else:
-            pl.when(chip != col)(lambda: basis_copy(col).wait_send())
+        pl.when(target < cuts)(lambda: cut_copy(target).wait_send())
+
+    @pl.when(relays)
+    def _():
+        for plane in range(chips):
+            pl.when(plane != chip)(lambda: line_copy(plane).wait_send())
+            for shift in range(1, cols):
+                spread_copy(relay.at[plane], plane, lax.rem(col + shift, cols)).wait_send()
 
     @pl.loop(0, steps)
     def _(step):
@@ -289,10 +347,11 @@
     def per_device(matrix, range_basis):
         depth, block = matrix.shape
         inner, vectors = range_basis.shape
-        assert chips == cols and inner == CORES * depth and block % WIDTH == 0
+        assert chips == cols >= -(-inner // 128) and inner == CORES * depth and block % WIDTH == 0
         steps = block // WIDTH
         ring = LEAD + SKEW * (chips - 1) + SPARE
-        padded = -(-inner // 128) * 128
+        cuts = -(-inner // 128)
+        padded = cuts * 128
         count = chips * vectors
         dma = pltpu.SemaphoreType.DMA
         return pl.pallas_call(
@@ -302,14 +361,19 @@
             out_specs=pl.BlockSpec(memory_space=pltpu.VMEM),
             scratch_shapes=[
                 pltpu.VMEM((vectors, inner), jnp.float32),
-                pltpu.VMEM((chips, vectors, inner), jnp.float32),
+                pltpu.VMEM((cuts, vectors, 128), jnp.float32),
+                pltpu.VMEM((cols, vectors, 128), jnp.float32),
+                pltpu.VMEM((chips, cuts, vectors, 128), jnp.float32),
                 pltpu.VMEM((2 * count, padded), jnp.bfloat16),
                 pltpu.VMEM((steps, inner, WIDTH), jnp.float32),
                 pltpu.VMEM((ring, count, WIDTH), jnp.float32),
                 pltpu.VMEM((chips + 1, steps, vectors, WIDTH), jnp.float32),
                 dma,
+                dma((cuts,)),
                 dma((cols,)),
                 dma((chips,)),
+                dma((chips, cols)),
+                dma((chips, cuts)),
                 dma((steps,)),
                 dma((steps,)),
                 dma((steps,)),

time: 253 us -> 235 us (0.929)
  Pallas kernels: 245 us -> 228 us
    pallas_call x1, Pallas kernels: 245 us -> 228 us  [per_device(): pl.pallas_call(functools.partial(kernel, chips, cols), out_shape=pltpu.VM...]
where the time goes in v2:
time: 235 us; the launch traced here: 233 us
  Pallas kernels  228 us (97%)
  local copies, waits for them, and re-layouts  4.78 us (2%)
    pallas_call x1, Pallas kernels, per_device(): pl.pallas_call(functools.partial(kernel, chips, cols), out_shape=pltpu.VM...  228 us
    unnamed x1, local copies, waits for them, and re-layouts  4.78 us

profile of v2, /device:TPU:0, one launch (start us, length us, event | category | flops | bytes accessed | tf_op | source)
XLA Modules:
  0.0 233.0 jit_solution(3071504452519894698)
XLA Ops:
  0.0 228.2 %shard_map.28 = f32[48,65536]{1,0:T(8,128)S(1)} custom-call(f32[48,432]{1,0:T(8,128)} %bitcast.1, f32[216,16384]{1,0:T(8,128)} %matrix_ref.1), custom_call_target="tpu_custom_call" | custom-call | tf_op jit(solution)/shard_map/pallas_call | solution.py:357
  228.2 4.8 %copy.4 = f32[48,65536]{1,0:T(8,128)} copy(f32[48,65536]{1,0:T(8,128)S(1)} %shard_map.28) | data formatting | bytes 25165824

commit v3 on v2

v3 whole, which is shorter than its diff:
```python
import functools

import jax
import jax.numpy as jnp
from jax import lax
from jax.experimental import pallas as pl
from jax.experimental.pallas import tpu as pltpu
from jax.sharding import PartitionSpec as P

MESH = pl.DeviceIdType.MESH
CORES = 2
WIDE = 1024
NARROW = 256
TILE = 512
TAPER = 2
LEAD = 2
SKEW = 1
SPARE = 1
AHEAD = 3


def split_parts(value):
    high = value.astype(jnp.bfloat16)
    return high, (value - high.astype(jnp.float32)).astype(jnp.bfloat16)


def dot(left, right):
    return jnp.dot(left, right, preferred_element_type=jnp.float32)


def kernel(
    chips, cols, basis_ref, matrix_ref, out_ref, loaded, cut, relay, basis, halves, rows, part, sums,
    lent_rows, lent_basis, lent_halves,
    basis_load, cut_send, cut_recv, line_send, spread_send, basis_recv, rows_local, rows_send, rows_recv,
    lent_send, lent_recv, lent_pass, lent_line, lent_spread, lent_basis_recv, sum_send, sum_recv, out_send, out_recv,
):
    row, col = lax.axis_index("row"), lax.axis_index("col")
    chip, core = row // CORES, row % CORES
    vectors, inner = basis_ref.shape
    depth, block = matrix_ref.shape
    count = chips * vectors
    wide = block // WIDE - TAPER
    steps = wide + TAPER * WIDE // NARROW
    first, last = chip == 0, chip == chips - 1
    ends = first | last
    ring = part.shape[0]
    lent = wide
    upper = chips - 2
    borrower = (chip == 1) | (chip == upper)
    lender = jnp.where(chip == 1, 0, chips - 1)

    def columns(step, size, base=0):
        start = jnp.where(step < wide, step * WIDE, wide * WIDE + (step - wide) * NARROW)
        return pl.ds(pl.multiple_of(base + start, NARROW), size)

    def sized(step, run):
        pl.when(step < wide)(lambda: run(WIDE))
        pl.when(step >= wide)(lambda: run(NARROW))

    def device(at_chip, at_col, at_core=core):
        return {"row": CORES * at_chip + at_core, "col": at_col}

    cuts = cut.shape[0]

    def cut_copy(target):
        return pltpu.make_async_remote_copy(
            src_ref=cut.at[target],
            dst_ref=relay.at[col],
            send_sem=cut_send.at[target],
            recv_sem=cut_recv.at[col],
            device_id=device(chip, target),
            device_id_type=MESH,
        )

    def cut_wait(source):
        pltpu.make_async_copy(cut.at[0], relay.at[source], cut_recv.at[source]).wait()

    def line_copy(plane):
        return pltpu.make_async_remote_copy(
            src_ref=relay.at[plane],
            dst_ref=basis.at[chip, col],
            send_sem=line_send.at[plane],
            recv_sem=basis_recv.at[chip, col],
            device_id=device(plane, col),
            device_id_type=MESH,
        )

    def spread_copy(source, owner, target):
        return pltpu.make_async_remote_copy(
            src_ref=source,
            dst_ref=basis.at[owner, col],
            send_sem=spread_send.at[owner, target],
            recv_sem=basis_recv.at[owner, col],
            device_id=device(chip, target),
            device_id_type=MESH,
        )

    def basis_wait(owner, at):
        pltpu.make_async_copy(cut.at[0], basis.at[owner, at], basis_recv.at[owner, at]).wait()

    def rows_own(step, size):
        return pltpu.make_async_copy(
            matrix_ref.at[:, columns(step, size)],
            rows.at[pl.ds(core * depth, depth), columns(step, size)],
            rows_local.at[step],
        )

    def rows_peer(step, size, owner):
        return pltpu.make_async_remote_copy(
            src_ref=matrix_ref.at[:, columns(step, size)],
            dst_ref=rows.at[pl.ds(owner * depth, depth), columns(step, size)],
            send_sem=rows_send.at[step],
            recv_sem=rows_recv.at[step],
            device_id=device(chip, col, 1 - core),
            device_id_type=MESH,
        )

    def lend():
        return pltpu.make_async_remote_copy(
            src_ref=matrix_ref.at[:, columns(lent, NARROW)],
            dst_ref=lent_rows.at[pl.ds(core * depth, depth)],
            send_sem=lent_send,
            recv_sem=lent_recv.at[core],
            device_id=device(jnp.where(first, 1, upper), col),
            device_id_type=MESH,
        )

    def lend_peer(owner):
        return pltpu.make_async_remote_copy(
            src_ref=lent_rows.at[pl.ds(core * depth, depth)],
            dst_ref=lent_rows.at[pl.ds(owner * depth, depth)],
            send_sem=lent_pass,
            recv_sem=lent_recv.at[owner],
            device_id=device(chip, col, 1 - core),
            device_id_type=MESH,
        )

    def lent_line_copy(plane, towards):
        return pltpu.make_async_remote_copy(
            src_ref=relay.at[plane],
            dst_ref=lent_basis.at[chip, col],
            send_sem=lent_line.at[min(plane, 1)],
            recv_sem=lent_basis_recv.at[chip, col],
            device_id=device(towards, col),
            device_id_type=MESH,
        )

    def lent_spread_copy(source, owner, target):
        return pltpu.make_async_remote_copy(
            src_ref=source,
            dst_ref=lent_basis.at[owner, col],
            send_sem=lent_spread.at[owner, target],
            recv_sem=lent_basis_recv.at[owner, col],
            device_id=device(chip, target),
            device_id_type=MESH,
        )

    def lent_wait(owner, at):
        pltpu.make_async_copy(cut.at[0], lent_basis.at[owner, at], lent_basis_recv.at[owner, at]).wait()

    def sum_at(slot, step, size):
        return sums.at[slot, :, columns(step, size)]

    def sum_copy(source, owner, slot, step, size, towards):
        return pltpu.make_async_remote_copy(
            src_ref=source,
            dst_ref=sum_at(slot, step, size),
            send_sem=sum_send.at[owner, step],
            recv_sem=sum_recv.at[slot, step],
            device_id=device(towards, col),
            device_id_type=MESH,
        )

    def owned(owner):
        return pl.ds(pl.multiple_of(owner * vectors, vectors), vectors)

    def part_of(step, size, owner):
        return part.at[lax.rem(step, ring), owned(owner), pl.ds(0, size)]

    def send_up(source, owner, step, size):
        sum_copy(source, owner, owner, step, size, chip + 1).start()

    def send_down(source, owner, step, size):
        slot = jnp.where(owner == chip - 1, chips, owner)
        sum_copy(source, owner, slot, step, size, chip - 1).start()

    neighbour = jnp.where(first, 1, chip - 1)

    def sum_wait(slot, step, size):
        sum_copy(sum_at(slot, step, size), 0, slot, step, size, neighbour).wait_recv()

    def sums_sent(step, size):
        for owner in range(chips):

            @pl.when(owner != chip)
            def _():
                sum_copy(sum_at(owner, step, size), owner, owner, step, size, neighbour).wait_send()

    def out_at(step, size, owner):
        return out_ref.at[:, columns(step, size, owner * block)]

    def out_copy(step, size, target, owner):
        return pltpu.make_async_remote_copy(
            src_ref=out_at(step, size, col),
            dst_ref=out_at(step, size, owner),
            send_sem=out_send.at[target, step],
            recv_sem=out_recv.at[owner, step],
            device_id=device(chip, target),
            device_id_type=MESH,
        )

    load = pltpu.make_async_copy(basis_ref, loaded, basis_load)
    load.start()
    for step in range(AHEAD):
        rows_own(step, WIDE).start()

    barrier = pltpu.get_barrier_semaphore()

    def greet(where):
        pl.semaphore_signal(barrier, inc=1, device_id=where, device_id_type=MESH)

    for plane in range(chips):
        pl.when(plane != chip)(lambda: greet(device(plane, col)))
    for shift in range(1, cols):
        greet(device(chip, lax.rem(col + shift, cols)))
    greet(device(chip, col, 1 - core))
    load.wait()
    for at in range(cuts):
        size = min(128, inner - at * 128)
        cut[at, :, :size] = loaded[:, at * 128 : at * 128 + size]
        if size < 128:
            cut[at, :, size:] = jnp.zeros((vectors, 128 - size), jnp.float32)

    relays = col < cuts

    @pl.when(relays)
    def _():
        relay[col] = cut[lax.rem(col, cuts)]

    pl.semaphore_wait(barrier, chips + cols - 1)

    for shift in range(1, cols):
        target = lax.rem(col + shift, cols)
        pl.when(target < cuts)(lambda: cut_copy(target).start())
    pl.when(ends)(lambda: lend().start())
    rows_peer(0, WIDE, core).start()

    low_half = chip < chips // 2
    way = jnp.where(low_half, 1, chips - 1)

    @pl.when(relays)
    def _():
        for hop in range(chips):
            plane = jnp.where(low_half, hop, chips - 1 - hop)
            pl.when(plane != col)(lambda: cut_wait(plane))
            pl.when(plane != chip)(lambda: line_copy(plane).start())

    rows_peer(1, WIDE, core).start()

    @pl.when(relays)
    def _():
        for hop in range(1, chips + 1):
            owner = lax.rem(chip + hop * way, chips)
            if hop < chips:
                basis_wait(owner, col)
            else:
                basis[owner, col] = relay[owner]
            source = basis.at[owner, col] if hop < chips else relay.at[owner]
            for shift in range(1, cols):
                spread_copy(source, owner, lax.rem(col + shift, cols)).start()

    loans = ((0, 1), (chips - 1, upper))

    @pl.when(relays)
    def _():
        for plane, towards in loans:
            pl.when((chip != plane) & (chip != towards))(lambda: lent_line_copy(plane, towards).start())

    for step in range(2, AHEAD):
        rows_peer(step, WIDE, core).start()

    def fetch(step):
        def run(size):
            rows_own(step, size).start()
            rows_peer(step, size, core).start()

        pl.when(step < steps)(lambda: sized(step, run))

    def rows_ready(step, size):
        rows_own(step, size).wait()
        rows_peer(step, size, 1 - core).wait_recv()

    def tiles(size, body):
        if size <= TILE:
            body(0)
        else:
            pl.loop(0, size // TILE)(lambda at: body(pl.multiple_of(at * TILE, TILE)))

    def product(left, right, size):
        value, rest = split_parts(right)
        both = dot(left[:, :inner], value)
        third = dot(left[:count, :inner], rest)
        return both[:count] + (both[count:] + third)

    for hop in range(1, chips + 1):
        owner = lax.rem(chip + hop * way, chips)
        for at in range(cuts):
            pl.when(col != at)(lambda: basis_wait(owner, at))

        @pl.loop(0, LEAD)
        def _(step):
            if hop == 1:
                rows_ready(step, WIDE)

            @functools.partial(tiles, WIDE)
            def _(at):
                right, rest = split_parts(rows[:, pl.ds(pl.multiple_of(step * WIDE + at, TILE), TILE)])
                mine = jnp.concatenate([basis[owner, at] for at in range(cuts)], axis=1)
                high, low = split_parts(mine[:, :inner])
                part[step, owned(owner), pl.ds(at, TILE)] = dot(high, right) + (dot(low, right) + dot(high, rest))

            if hop < chips:
                pl.when(first)(lambda: send_up(part_of(step, WIDE, owner), owner, step, WIDE))
                pl.when(last)(lambda: send_down(part_of(step, WIDE, owner), owner, step, WIDE))

    whole = [basis[:, at].reshape(count, 128) for at in range(cuts)]
    high, low = split_parts(jnp.concatenate(whole, axis=1))
    halves[:count] = high
    halves[count:] = low

    @pl.when(borrower)
    def _():
        lend_peer(core).wait_recv()
        lend_peer(core).start()

        @pl.when(relays)
        def _():
            lent_basis[chip, col] = relay[lender]
            for owner in range(chips):

                @pl.when(owner != lender)
                def _():
                    pl.when(owner != chip)(lambda: lent_wait(owner, col))
                    for shift in range(1, cols):
                        lent_spread_copy(lent_basis.at[owner, col], owner, lax.rem(col + shift, cols)).start()

        lent_basis[lender] = jnp.zeros((cuts, vectors, 128), jnp.float32)

    def compute(step, size):
        fetch(step + AHEAD - LEAD)
        rows_ready(step, size)
        slot = lax.rem(step, ring)
        old = step - ring

        @pl.when(ends & (old >= 0) & (old != lent))
        def _():
            sized(old, functools.partial(sums_sent, old))

        span = min(size, TILE)

        @functools.partial(tiles, size)
        def _(at):
            lanes = columns(step, span, at)
            part[slot, :, pl.ds(at, span)] = product(halves, rows[:, lanes], span)

        if size == NARROW:

            @pl.when(borrower & (step == lent))
            def _():
                for owner in range(chips):
                    for at in range(cuts):
                        pl.when((owner != lender) & (col != at))(lambda: lent_wait(owner, at))
                whole = [lent_basis[:, at].reshape(count, 128) for at in range(cuts)]
                high, low = split_parts(jnp.concatenate(whole, axis=1))
                lent_halves[:count] = high
                lent_halves[count:] = low
                lend_peer(1 - core).wait_recv()
                part[slot, :, pl.ds(0, size)] += product(lent_halves, lent_rows[...], size)

    def launch(tick):
        for far in range(chips - 1):
            step = tick - SKEW * far

            def run(size):
                up, down = chips - 1 - far, far
                pl.when(first)(lambda: send_up(part_of(step, size, up), up, step, size))
                pl.when(last)(lambda: send_down(part_of(step, size, down), down, step, size))

            @pl.when(ends & (step >= LEAD) & (step < steps) & (step != lent))
            def _():
                sized(step, run)

    def forward(owner, step, send, nearest):
        given = (step == lent) & (chip == nearest)

        def run(size):
            here = columns(step, size)

            @pl.when(given)
            def _():
                sums[owner, :, here] = part_of(step, size, owner)[...]

            @pl.when(jnp.logical_not(given))
            def _():
                sum_wait(owner, step, size)
                sums[owner, :, here] = sums[owner, :, here] + part_of(step, size, owner)[...]

            send(sum_at(owner, step, size), owner, step, size)

        pl.when((step >= 0) & (step < steps))(lambda: sized(step, run))

    def finish(step, size):
        total = part_of(step, size, chip)

        def add(slot):
            sum_wait(slot, step, size)
            total[...] += sums[slot, :, columns(step, size)]

        pl.when((chip > 0) & ((step != lent) | (chip != 1)))(lambda: add(chip))
        pl.when((chip < chips - 1) & ((step != lent) | (chip != upper)))(lambda: add(chips))
        out_ref[:, columns(step, size, col * block)] = total[...]
        for shift in range(1, cols):
            out_copy(step, size, lax.rem(col + shift, cols), col).start()

    @pl.loop(0, steps + SKEW * (chips - 1))
    def _(turn):
        ahead = turn + LEAD
        pl.when(ahead < steps)(lambda: sized(ahead, functools.partial(compute, ahead)))
        launch(ahead)

        for owner in range(chips - 1, 0, -1):
            step = turn - SKEW * (chip + chips - 1 - owner)
            pl.when((chip > 0) & (chip < owner))(lambda: forward(owner, step, send_up, 1))
            down = chips - 1 - owner
            back = turn - SKEW * (chips - 1 - chip + down)
            pl.when((chip < chips - 1) & (chip > down))(lambda: forward(down, back, send_down, upper))

        done = turn - SKEW * (chips - 1)
        pl.when(done >= 0)(lambda: sized(done, functools.partial(finish, done)))

    for shift in range(1, cols):
        target = lax.rem(col + shift, cols)
        pl.when(target < cuts)(lambda: cut_copy(target).wait_send())

    @pl.when(relays)
    def _():
        for plane in range(chips):
            pl.when(plane != chip)(lambda: line_copy(plane).wait_send())
            for shift in range(1, cols):
                spread_copy(relay.at[plane], plane, lax.rem(col + shift, cols)).wait_send()
        for plane, towards in loans:
            pl.when((chip != plane) & (chip != towards))(lambda: lent_line_copy(plane, towards).wait_send())

        @pl.when(borrower)
        def _():
            for owner in range(chips):
                for shift in range(1, cols):
                    target = lax.rem(col + shift, cols)
                    pl.when(owner != lender)(lambda: lent_spread_copy(relay.at[0], owner, target).wait_send())

    pl.when(ends)(lambda: lend().wait_send())
    pl.when(borrower)(lambda: lend_peer(core).wait_send())

    def drain(step, size):
        rows_peer(step, size, core).wait_send()
        left = jnp.logical_not(ends) | ((step >= steps - ring) & (step != lent))
        pl.when(left)(lambda: sums_sent(step, size))
        for shift in range(1, cols):
            other = lax.rem(col + shift, cols)
            out_copy(step, size, other, col).wait_send()
            out_copy(step, size, other, other).wait_recv()

    pl.loop(0, wide)(lambda step: drain(step, WIDE))
    pl.loop(wide, steps)(lambda step: drain(step, NARROW))


def solution(mesh):
    chips, cols = mesh.shape["row"] // CORES, mesh.shape["col"]

    def per_device(matrix, range_basis):
        depth, block = matrix.shape
        inner, vectors = range_basis.shape
        assert chips >= 4 and chips == cols >= -(-inner // 128) and inner == CORES * depth and block % WIDE == 0
        steps = block // WIDE - TAPER + TAPER * WIDE // NARROW
        ring = LEAD + SKEW * (chips - 1) + SPARE
        cuts = -(-inner // 128)
        padded = cuts * 128
        count = chips * vectors
        dma = pltpu.SemaphoreType.DMA
        return pl.pallas_call(
            functools.partial(kernel, chips, cols),
            out_shape=pltpu.VMEM((vectors, cols * block), jnp.float32),
            in_specs=[pl.BlockSpec(memory_space=pl.ANY)] * 2,
            out_specs=pl.BlockSpec(memory_space=pltpu.VMEM),
            scratch_shapes=[
                pltpu.VMEM((vectors, inner), jnp.float32),
                pltpu.VMEM((cuts, vectors, 128), jnp.float32),
                pltpu.VMEM((cols, vectors, 128), jnp.float32),
                pltpu.VMEM((chips, cuts, vectors, 128), jnp.float32),
                pltpu.VMEM((2 * count, padded), jnp.bfloat16),
                pltpu.VMEM((inner, block), jnp.float32),
                pltpu.VMEM((ring, count, WIDE), jnp.float32),
                pltpu.VMEM((chips + 1, vectors, block), jnp.float32),
                pltpu.VMEM((inner, NARROW), jnp.float32),
                pltpu.VMEM((chips, cuts, vectors, 128), jnp.float32),
                pltpu.VMEM((2 * count, padded), jnp.bfloat16),
                dma,
                dma((cuts,)),
                dma((cols,)),
                dma((chips,)),
                dma((chips, cols)),
                dma((chips, cuts)),
                dma((steps,)),
                dma((steps,)),
                dma((steps,)),
                dma,
                dma((CORES,)),
                dma,
                dma((2,)),
                dma((chips, cols)),
                dma((chips, cuts)),
                dma((chips, steps)),
                dma((chips + 1, steps)),
                dma((cols, steps)),
                dma((cols, steps)),
            ],
            compiler_params=pltpu.CompilerParams(
                has_side_effects=True, collective_id=0, vmem_limit_bytes=54_000_000
            ),
        )(range_basis.T, matrix)

    return jax.shard_map(
        per_device,
        mesh=mesh,
        in_specs=(P("row", "col"), P("col", "row")),
        out_specs=P("row", None),
        check_vma=False,
    )
```

time: 235 us -> 231 us (0.983)
  no operation moved by 1% of the time
where the time goes in v3:
time: 231 us
  Pallas kernels  226 us (98%)
  local copies, waits for them, and re-layouts  4.78 us (2%)
    pallas_call x1, Pallas kernels, per_device(): pl.pallas_call(functools.partial(kernel, chips, cols), out_shape=pltpu.VM...  226 us
    unnamed x1, local copies, waits for them, and re-layouts  4.78 us

profile of v3, /device:TPU:0, one launch (start us, length us, event | category | flops | bytes accessed | tf_op | source)
XLA Modules:
  0.0 231.2 jit_solution(4314431741298676568)
XLA Ops:
  0.0 226.4 %shard_map.28 = f32[48,65536]{1,0:T(8,128)S(1)} custom-call(f32[48,432]{1,0:T(8,128)} %bitcast.1, f32[216,16384]{1,0:T(8,128)} %matrix_ref.1), custom_call_target="tpu_custom_call" | custom-call | tf_op jit(solution)/shard_map/pallas_call | solution.py:490
  226.4 4.8 %copy.4 = f32[48,65536]{1,0:T(8,128)} copy(f32[48,65536]{1,0:T(8,128)S(1)} %shard_map.28) | data formatting | bytes 25165824

commit v4 on v3

--- a/solution.py
+++ b/solution.py
@@ -10,9 +10,9 @@
 MESH = pl.DeviceIdType.MESH
 CORES = 2
 WIDE = 1024
-NARROW = 256
+NARROW = 384
 TILE = 512
-TAPER = 2
+TAPER = 3
 LEAD = 2
 SKEW = 1
 SPARE = 1
@@ -51,7 +51,7 @@
 
     def columns(step, size, base=0):
         start = jnp.where(step < wide, step * WIDE, wide * WIDE + (step - wide) * NARROW)
-        return pl.ds(pl.multiple_of(base + start, NARROW), size)
+        return pl.ds(pl.multiple_of(base + start, 128), size)
 
     def sized(step, run):
         pl.when(step < wide)(lambda: run(WIDE))

time: 231 us -> 230 us (level)
  no operation moved by 1% of the time
where the time goes in v4:
time: 230 us
  Pallas kernels  225 us (98%)
  local copies, waits for them, and re-layouts  4.78 us (2%)
    pallas_call x1, Pallas kernels, per_device(): pl.pallas_call(functools.partial(kernel, chips, cols), out_shape=pltpu.VM...  225 us
    unnamed x1, local copies, waits for them, and re-layouts  4.78 us

profile of v4, /device:TPU:0, one launch (start us, length us, event | category | flops | bytes accessed | tf_op | source)
XLA Modules:
  0.0 230.1 jit_solution(3127289873039460666)
XLA Ops:
  0.0 225.3 %shard_map.28 = f32[48,65536]{1,0:T(8,128)S(1)} custom-call(f32[48,432]{1,0:T(8,128)} %bitcast.1, f32[216,16384]{1,0:T(8,128)} %matrix_ref.1), custom_call_target="tpu_custom_call" | custom-call | tf_op jit(solution)/shard_map/pallas_call | solution.py:490
  225.3 4.8 %copy.4 = f32[48,65536]{1,0:T(8,128)} copy(f32[48,65536]{1,0:T(8,128)S(1)} %shard_map.28) | data formatting | bytes 25165824
